TPU v7x, 32 devices: a whole 2x2x4 slice. The times are simulated.
32 devices in a mesh: outer: 4 (over y, x), inner: 8 (over z, core).
Axes of the slice: x: 2, y: 2, z: 4, core: 2. Of those that a mesh axis runs over, the one named last changes fastest.
Arguments:
- acts: bfloat16 [32, 2, 512, 512], P(('outer', 'inner')), may hold values from -6 to 6
- cotangent: bfloat16 [32, 2, 512, 512], P(('outer', 'inner')), may hold values from -6 to 6
- residual: float32 [32, 2048, 128], P(('outer', 'inner')), may hold values from -0.6 to 0.6
- owner_residual: float32 [32, 256, 128], P(('outer', 'inner')), may hold values from -3 to 3
- in_count: int32 [32, 2, 8], P(('outer', 'inner')), may hold values from 1 to 128, as said below
- in_rank: int32 [32, 2, 2048], P(('outer', 'inner')), may hold values from 0 to 255, as said below
- out_count: int32 [32, 2], P(('outer', 'inner')), may hold values from 1 to 128
- out_rank: int32 [32, 2, 256], P(('outer', 'inner')), may hold values from 0 to 255, as said below
Outputs:
- applied: bfloat16 [512, 512], replicated
- new_residual: float32 [32, 2048, 128], P(('outer', 'inner'))
- new_owner_residual: float32 [32, 256, 128], P(('outer', 'inner'))
Inputs may be any that keep to these rules, and one draw needn't show every extreme that they name: `in_count`: each step has one owner that receives 128 blocks from every replica. `in_rank`: for each replica, step and owner, the ranks of that owner's 256 blocks are a permutation of 0 to 255. `out_rank`: for each replica and step a permutation of 0 to 255.
All inputs are finite; a program needn't handle non-finite values.
Results may differ from a plain program's by a relative error of at most 0.0065.
Values may be sent and summed in bfloat16 or wider, within the bound.
A program may use at most 64 MiB of HBM per device.

v0:
```python
import math
import jax
import jax.numpy as jnp
from jax import lax
from jax.sharding import PartitionSpec as P

step_size = 0.0625


def select_blocks(resid, grad, ranks_flat, counts, owners, region, width):
    blocks = resid.shape[0]
    accum = (resid + grad.reshape(blocks, width)).reshape(owners, region, width)
    ranks = ranks_flat.reshape(owners, region)
    chosen = (ranks < counts[:, None])[..., None]
    new_resid = jnp.where(chosen, jnp.float32(0.0), accum).reshape(blocks, width)
    return (accum, ranks, chosen, new_resid)


def pack_slots(accum, ranks, counts, slots, region):
    order = lax.iota(jnp.int32, slots)
    picks = (ranks[:, None, :] == order[None, :, None]) & (
        order[None, :, None] < counts[:, None, None]
    )
    picks_f = picks.astype(jnp.float32)
    places = lax.iota(jnp.int32, region).astype(jnp.float32)
    packed = jnp.einsum("nkr,nrd->nkd", picks_f, accum, precision=lax.Precision.HIGHEST)
    where_at = jnp.einsum("nkr,r->nk", picks_f, places, precision=lax.Precision.HIGHEST)
    return (packed, where_at)


def unpack_slots(arrived, spots, region, width):
    places = lax.iota(jnp.int32, region).astype(jnp.float32)
    placed = (spots.reshape(-1)[:, None] == places[None, :]).astype(jnp.float32)
    return jnp.einsum(
        "mr,md->rd", placed, arrived.reshape(-1, width), precision=lax.Precision.HIGHEST
    )


def owner_section(pod_sum, oresid, ranks_out, count_out):
    owner_acc = pod_sum + oresid
    passed = (ranks_out < count_out)[:, None]
    outgoing = jnp.where(passed, owner_acc, jnp.float32(0.0))
    kept = jnp.where(passed, jnp.float32(0.0), owner_acc)
    return (outgoing, kept)


def per_device(acts, cotangent, residual, owner_residual, in_count, in_rank, out_count, out_rank):
    owners = lax.axis_size("inner")
    steps = acts.shape[1]
    tokens = acts.shape[2]
    rows = acts.shape[3]
    cols = cotangent.shape[3]
    blocks = residual.shape[1]
    width = residual.shape[2]
    region = blocks // owners
    slots = max(1, region // 2)
    scale = 1.0 / math.sqrt(tokens * owners)
    resid = residual[0]
    oresid = owner_residual[0]
    crosses = []
    packs = []
    spots_all = []
    for step in range(steps):
        grad = (
            jnp.einsum(
                "tr,tc->rc", acts[0, step], cotangent[0, step], preferred_element_type=jnp.float32
            )
            * scale
        )
        counts = in_count[0, step]
        accum, ranks, chosen, resid = select_blocks(
            resid, grad, in_rank[0, step], counts, owners, region, width
        )
        packed, where_at = pack_slots(accum, ranks, counts, slots, region)
        packs.append(packed)
        spots_all.append(where_at)
    arrived, spots = (
        lax.all_to_all(
            jnp.concatenate(packs, axis=1), "inner", split_axis=0, concat_axis=0, tiled=True
        ),
        lax.all_to_all(
            jnp.concatenate(spots_all, axis=1), "inner", split_axis=0, concat_axis=0, tiled=True
        ),
    )
    outgoings = []
    for step in range(steps):
        pod_sum = unpack_slots(
            arrived[:, step * slots : (step + 1) * slots],
            spots[:, step * slots : (step + 1) * slots],
            region,
            width,
        )
        outgoing, oresid = owner_section(pod_sum, oresid, out_rank[0, step], out_count[0, step])
        outgoings.append(outgoing)
    summed = lax.psum(jnp.stack(outgoings), "outer")
    for step in range(steps):
        crosses.append(summed[step])
    deltas = []
    for cross in crosses:
        delta = cross.astype(jnp.bfloat16)
        deltas.append(lax.all_gather(delta, "inner", axis=0, tiled=True))
    total = deltas[0].astype(jnp.float32)
    for later in deltas[1:]:
        total = total + later.astype(jnp.float32)
    applied = (-step_size * total).astype(jnp.bfloat16)
    return (applied.reshape(rows, cols), resid[None], oresid[None])


def solution(mesh):
    return jax.shard_map(
        per_device,
        mesh=mesh,
        in_specs=(
            P(("outer", "inner"), None, None, None),
            P(("outer", "inner"), None, None, None),
            P(("outer", "inner"), None, None),
            P(("outer", "inner"), None, None),
            P(("outer", "inner"), None, None),
            P(("outer", "inner"), None, None),
            P(("outer", "inner"), None),
            P(("outer", "inner"), None, None),
        ),
        out_specs=(P(), P(("outer", "inner"), None, None), P(("outer", "inner"), None, None)),
        check_vma=False,
    )
```

profile of v0, /device:TPU:0, one launch (start us, length us, event | category | flops | bytes accessed | tf_op | source)
XLA Modules:
  0.0 107.5 jit_solution(2119383466452367216)
XLA Ops:
  0.6 0.0 copy-start.8
  0.6 0.0 copy-start.9
  0.7 0.6 copy-done.8
  1.3 0.8 slice_reduce_fusion.1
  2.2 0.1 iota_compare_fusion.2
  2.3 0.6 fusion.6
  2.9 0.6 fusion.10
  3.5 0.6 all_to_all.11
  4.1 6.4 %all-to-all-start = ((f32[8,1,256]{2,1,0:T(1,128)}), f32[8,1,256]{2,1,0:T(1,128)S(1)}, u32[]{:S(2)}, u32[]{:S(2)}) async-start(f32[8,1,256]{2,1,0:T(1,128)} %all_to_all.11), calls=%async_computation | async-start | bytes 16384 | tf_op jit(solution)/shard_map/all_to_all | solution.py:81
  10.5 0.1 broadcast_compare_fusion
  10.6 0.0 copy-done.9
  10.6 1.6 %convolution_multiply_fusion = f32[512,512]{1,0:T(8,128)S(1)} fusion(bf16[1,2,512,512]{3,2,1,0:T(8,128)(2,1)S(1)} %copy-done.9, bf16[1,2,512,512]{3,2,1,0:T(8,128)(2,1)} %param.8), kind=kOutput, calls=%fused_computation | convolution fusion | flops 268697600 | bytes 2097152 | tf_op jit(solution)/shard_map/tr,tc->rc/dot_general | solution.py:65
  12.2 0.0 copy-done.10
  12.2 0.0 copy-start.1
  12.2 0.5 convolution_multiply_fusion.1
  12.7 0.0 copy-start.2
  12.7 1.0 copy-done.2
  13.7 0.1 reshape.167
  13.7 0.0 copy-done.1
  13.7 0.0 copy-start
  13.8 1.0 reshape.168
  14.8 0.6 copy-done
  15.4 0.9 fusion.4
  16.3 0.3 copy-done.4
  16.6 1.6 %fusion = f32[8,128,128]{2,1,0:T(8,128)S(1)} fusion(f32[8,256,128]{2,1,0:T(8,128)S(1)} %copy-done.4, s32[8,256]{1,0:T(8,128)S(1)} %eq.64, pred[8,256]{1,0:T(8,128)(4,1)S(1)} %broadcast_compare_fusion, pred[8,128]{1,0:T(8,128)(4,1)S(1)} %get-tuple-element.23, f32[8,256,128]{2,1,0:T(8,128)S(1)} %bitcast.55, f32[8,256,128]{2,1,0:T(8,128)S(1)} %reshape.167), kind=kOutput, calls=%fused_computation.7 | convolution fusion | flops 403963904 | bytes 3681280 | tf_op jit(solution)/shard_map/nkr,nrd->nkd/dot_general | solution.py:26
  18.2 1.1 pad_maximum_fusion
  19.3 0.0 all-to-all-done
  19.3 5.2 %all-to-all-start.1 = ((f32[8,256,128]{2,1,0:T(8,128)}), f32[8,256,128]{2,1,0:T(8,128)}, u32[]{:S(2)}, u32[]{:S(2)}) async-start(f32[8,256,128]{2,1,0:T(8,128)} %pad_maximum_fusion), calls=%async_computation.1 | async-start | bytes 2097152 | tf_op jit(solution)/shard_map/all_to_all | solution.py:78
  24.5 0.1 reshape.172
  24.6 1.3 %reshape.173 = f32[1,2048,128]{2,1,0:T(8,128)S(1)} reshape(f32[512,512]{1,0:T(8,128)} %copy-done.1) | data formatting | bytes 2097152 | tf_op jit(solution)/shard_map/reshape | solution.py:12
  25.9 0.1 broadcast_bitcast_fusion
  26.0 0.0 copy-start.7
  26.0 0.6 copy-done.7
  26.7 0.6 fusion.41
  27.2 0.7 copy-done.6
  27.9 1.3 %compare_reduce_fusion = (pred[256]{0:T(512)(128)(4,1)S(1)}, pred[256]{0:T(512)(128)(4,1)S(1)}) fusion(s32[1,2,256]{2,1,0:T(2,128)S(1)} %copy-done.6, s32[]{:T(128)} %bitcast.18, s32[]{:T(128)} %bitcast), kind=kLoop, calls=%fused_computation.56 | loop fusion | flops 512 | bytes 2568 | tf_op jit(solution)/shard_map/lt | solution.py:41
  29.2 2.4 %add_select_fusion = f32[1,2048,128]{2,1,0:T(8,128)} fusion(f32[1,2048,128]{2,1,0:T(8,128)S(1)} %reshape.173, f32[1,2048,128]{2,1,0:T(8,128)S(1)} %copy-done, f32[1,2048,128]{2,1,0:T(8,128)S(1)} %reshape.172, pred[2048]{0:T(1024)(128)(4,1)S(1)} %lt.117, pred[2048]{0:T(1024)(128)(4,1)S(1)} %lt.115), kind=kLoop, calls=%fused_computation.6 | loop fusion | flops 1048576 | bytes 4198400 | tf_op jit(solution)/shard_map/jit(_where)/select_n | solution.py:15
  31.7 19.5 %all-to-all-done.1 = f32[8,256,128]{2,1,0:T(8,128)} async-done(((f32[8,256,128]{2,1,0:T(8,128)}), f32[8,256,128]{2,1,0:T(8,128)}, u32[]{:S(2)}, u32[]{:S(2)}) %all-to-all-start.1) | async-done | bytes 1048608 | tf_op jit(solution)/shard_map/all_to_all | solution.py:78
  51.2 1.3 %fusion.39 = (f32[8,128,128]{2,1,0:T(8,128)S(1)}, f32[8,128,128]{2,1,0:T(8,128)S(1)}) fusion(f32[8,256,128]{2,1,0:T(8,128)} %all-to-all-done.1), kind=kLoop, calls=%fused_computation.64 | loop fusion | bytes 2097152 | tf_op jit(solution)/shard_map/slice | solution.py:88
  52.5 0.0 copy-done.5
  52.5 1.2 %convolution_add_fusion.1 = f32[256,128]{1,0:T(8,128)S(1)} fusion(f32[1024,128]{1,0:T(8,128)S(1)} %bitcast.57, f32[256]{0:T(256)S(1)} %iota_convert_fusion, f32[1024]{0:T(1024)S(1)} %get-tuple-element.15, f32[1,256,128]{2,1,0:T(8,128)S(1)} %copy-done.5), kind=kOutput, calls=%fused_computation.3 | convolution fusion | flops 402948096 | bytes 791552 | tf_op jit(solution)/shard_map/mr,md->rd/dot_general | solution.py:34
  53.7 0.1 select_bitcast_fusion.2
  53.8 1.8 %select_bitcast_fusion = (f32[1,256,128]{2,1,0:T(8,128)}, f32[1,256,128]{2,1,0:T(8,128)S(1)}) fusion(pred[256]{0:T(512)(128)(4,1)S(1)} %get-tuple-element.5, f32[256,128]{1,0:T(8,128)S(1)} %convolution_add_fusion.1, pred[256]{0:T(512)(128)(4,1)S(1)} %get-tuple-element.6, f32[1024,128]{1,0:T(8,128)S(1)} %bitcast.56, f32[256]{0:T(256)S(1)} %iota_convert_fusion, ...), kind=kOutput, calls=%fused_computation.44 | convolution fusion | flops 403046400 | bytes 923136 | tf_op jit(solution)/shard_map/mr,md->rd/dot_general | solution.py:34
  55.6 20.9 %all-reduce.1 = bf16[2,256,128]{2,1,0:T(8,128)(2,1)S(1)} all-reduce(f32[2,256,128]{2,1,0:T(8,128)S(1)} %pad_maximum_fusion.1), channel_id=1, replica_groups=mesh['outer'=4,'inner'=8] {'outer'}, use_global_device_ids=true, to_apply=%region_0.1 | all-reduce | flops 65536 | bytes 393216 | tf_op jit(solution)/shard_map/psum | solution.py:95
  76.5 14.8 %all-gather = bf16[1,2048,128]{2,1,0:T(8,128)(2,1)S(1)} all-gather(bf16[1,256,128]{2,1,0:T(8,128)(2,1)S(1)} %get-tuple-element.11), channel_id=2, replica_groups=mesh['outer'=4,'inner'=8] {'inner'}, dimensions={1}, use_global_device_ids=true | all-gather | bytes 589824 | tf_op jit(solution)/shard_map/all_gather | solution.py:101
  91.4 14.8 %all-gather.1 = bf16[1,2048,128]{2,1,0:T(8,128)(2,1)S(1)} all-gather(bf16[1,256,128]{2,1,0:T(8,128)(2,1)S(1)} %get-tuple-element.12), channel_id=3, replica_groups=mesh['outer'=4,'inner'=8] {'inner'}, dimensions={1}, use_global_device_ids=true | all-gather | bytes 589824 | tf_op jit(solution)/shard_map/all_gather | solution.py:101
  106.2 0.2 multiply_convert_fusion
  106.4 1.1 %reshape.171 = bf16[512,512]{1,0:T(8,128)(2,1)} reshape(bf16[1,2048,128]{2,1,0:T(8,128)(2,1)S(1)} %multiply_convert_fusion) | data formatting | bytes 1048576 | tf_op jit(solution)/shard_map/reshape | solution.py:106
  (19 shorter events, 0.1 us)
Async XLA Ops:
  0.6 0.7 copy-start.8
  0.6 9.9 %copy-start.9 = (bf16[1,2,512,512]{3,2,1,0:T(8,128)(2,1)S(1)}, bf16[1,2,512,512]{3,2,1,0:T(8,128)(2,1)}, u32[]{:S(2)}) copy-start(bf16[1,2,512,512]{3,2,1,0:T(8,128)(2,1)} %param.9) | copy-start | bytes 3145732
  4.1 15.1 %all-to-all-start = ((f32[8,1,256]{2,1,0:T(1,128)}), f32[8,1,256]{2,1,0:T(1,128)S(1)}, u32[]{:S(2)}, u32[]{:S(2)}) async-start(f32[8,1,256]{2,1,0:T(1,128)} %all_to_all.11), calls=%async_computation | async-start | bytes 16384 | tf_op jit(solution)/shard_map/all_to_all | solution.py:81
  10.6 1.6 %copy-start.10 = (bf16[1,2,512,512]{3,2,1,0:T(8,128)(2,1)S(1)}, bf16[1,2,512,512]{3,2,1,0:T(8,128)(2,1)}, u32[]{:S(2)}) copy-start(bf16[1,2,512,512]{3,2,1,0:T(8,128)(2,1)} %param.8) | copy-start | bytes 3145732
  12.2 1.6 %copy-start.1 = (f32[512,512]{1,0:T(8,128)}, f32[512,512]{1,0:T(8,128)S(1)}, u32[]{:S(2)}) copy-start(f32[512,512]{1,0:T(8,128)S(1)} %convolution_multiply_fusion) | copy-start | bytes 3145732
  12.7 1.0 copy-start.2
  13.7 1.6 %copy-start = (f32[1,2048,128]{2,1,0:T(8,128)S(1)}, f32[1,2048,128]{2,1,0:T(8,128)}, u32[]{:S(2)}) copy-start(f32[1,2048,128]{2,1,0:T(8,128)} %param.10) | copy-start | bytes 3145732
  15.4 1.2 %copy-start.4 = (f32[8,256,128]{2,1,0:T(8,128)S(1)}, f32[8,256,128]{2,1,0:T(8,128)}, u32[]{:S(2)}) copy-start(f32[8,256,128]{2,1,0:T(8,128)} %reshape.168) | copy-start | bytes 3145732
  19.3 5.2 %copy-start.3 = (f32[512,512]{1,0:T(8,128)S(1)}, f32[512,512]{1,0:T(8,128)}, u32[]{:S(2)}) copy-start(f32[512,512]{1,0:T(8,128)} %copy-done.2) | copy-start | bytes 3145732
  19.3 31.9 %all-to-all-start.1 = ((f32[8,256,128]{2,1,0:T(8,128)}), f32[8,256,128]{2,1,0:T(8,128)}, u32[]{:S(2)}, u32[]{:S(2)}) async-start(f32[8,256,128]{2,1,0:T(8,128)} %pad_maximum_fusion), calls=%async_computation.1 | async-start | bytes 2097152 | tf_op jit(solution)/shard_map/all_to_all | solution.py:78
  26.0 0.7 copy-start.7
  27.2 0.7 copy-start.6
  31.7 20.8 %copy-start.5 = (f32[1,256,128]{2,1,0:T(8,128)S(1)}, f32[1,256,128]{2,1,0:T(8,128)}, u32[]{:S(2)}) copy-start(f32[1,256,128]{2,1,0:T(8,128)} %param.11) | copy-start | bytes 393220
where the time goes:
time: 108 us; the launch traced here: 107 us
  blocking collectives  50.6 us (47%)
  waiting for transfers between devices  19.5 us (18%)
  starting transfers between devices  11.6 us (11%)
  local copies, waits for them, and re-layouts  10.9 us (10%)
  matrix products  8.8 us (8%)
  other arithmetic  5.26 us (5%)
    all_gather x2, blocking collectives, per_device(): deltas.append(lax.all_gather(delta, 'inner', axis=0, tiled=True))  29.6 us
    psum x1, blocking collectives, per_device(): summed = lax.psum(jnp.stack(outgoings), 'outer')  20.9 us
    all_to_all x1, waiting for transfers between devices, per_device(): lax.all_to_all(jnp.concatenate(packs, axis=1), 'inner', split_axis=0, con...  19.5 us
    all_to_all x1, starting transfers between devices, per_device(): lax.all_to_all(jnp.concatenate(spots_all, axis=1), 'inner', split_axis=0,...  6.35 us
    all_to_all x1, starting transfers between devices, per_device(): lax.all_to_all(jnp.concatenate(packs, axis=1), 'inner', split_axis=0, con...  5.23 us
    unnamed x26, local copies, waits for them, and re-layouts  3.94 us
    dot_general x2, matrix products, unpack_slots(): jnp.einsum('mr,md->rd', placed, arrived.reshape(-1, width), precision=lax...  2.97 us
    dot_general x2, matrix products, pack_slots(): jnp.einsum('nkr,nrd->nkd', picks_f, accum, precision=lax.Precision.HIGHEST)  2.51 us
  transfers between devices with their start and end apart: 2, of which 1 were waited for; matrix products, arithmetic and copies ran while one was open for 12% of the time, Pallas kernels for 0%

commit v1 on v0

--- a/solution.py
+++ b/solution.py
@@ -92,7 +92,7 @@
         )
         outgoing, oresid = owner_section(pod_sum, oresid, out_rank[0, step], out_count[0, step])
         outgoings.append(outgoing)
-    summed = lax.psum(jnp.stack(outgoings), "outer")
+    summed = jnp.sum(lax.all_gather(jnp.stack(outgoings), "outer"), axis=0)
     for step in range(steps):
         crosses.append(summed[step])
     deltas = []

time: 108 us -> 127 us (1.18)
  waiting for transfers between devices: 19.5 us -> 45.6 us
  blocking collectives: 50.6 us -> 29.5 us
  between operations: 0.85 us -> 14.3 us
  other arithmetic: 5.26 us -> 7.23 us
  local copies, waits for them, and re-layouts: 10.9 us -> 9.02 us
    all_gather x0 -> x1, waiting for transfers between devices: none -> 21.7 us  [per_device(): summed = jnp.sum(lax.all_gather(jnp.stack(outgoings), 'outer'), axis=0)]
    psum x1 -> x0, blocking collectives: 20.9 us -> none  [per_device(): summed = lax.psum(jnp.stack(outgoings), 'outer')]
    all_to_all x1, waiting for transfers between devices: 19.5 us -> 23.9 us  [per_device(): lax.all_to_all(jnp.concatenate(packs, axis=1), 'inner', split_axis=0, con...]
    reduce_sum x0 -> x1, other arithmetic: none -> 1.29 us  [per_device(): summed = jnp.sum(lax.all_gather(jnp.stack(outgoings), 'outer'), axis=0)]
  transfers between devices with their start and end apart: 2 -> 3, of which waited for: 1 -> 2; matrix products, arithmetic and copies ran while one was open for 12% -> 10% of each run, Pallas kernels for 0% -> 0%
where the time goes in v1:
time: 127 us; the launch traced here: 126 us
  waiting for transfers between devices  45.6 us (36%)
  blocking collectives  29.5 us (23%)
  between operations  14.3 us (11%)
  starting transfers between devices  11.6 us (9%)
  local copies, waits for them, and re-layouts  9.02 us (7%)
  matrix products  8.8 us (7%)
  other arithmetic  7.23 us (6%)
    all_gather x2, blocking collectives, per_device(): deltas.append(lax.all_gather(delta, 'inner', axis=0, tiled=True))  29.5 us
    all_to_all x1, waiting for transfers between devices, per_device(): lax.all_to_all(jnp.concatenate(packs, axis=1), 'inner', split_axis=0, con...  23.9 us
    all_gather x1, waiting for transfers between devices, per_device(): summed = jnp.sum(lax.all_gather(jnp.stack(outgoings), 'outer'), axis=0)  21.7 us
    all_to_all x1, starting transfers between devices, per_device(): lax.all_to_all(jnp.concatenate(spots_all, axis=1), 'inner', split_axis=0,...  6.35 us
    all_to_all x1, starting transfers between devices, per_device(): lax.all_to_all(jnp.concatenate(packs, axis=1), 'inner', split_axis=0, con...  5.23 us
    unnamed x26, local copies, waits for them, and re-layouts  3.29 us
    dot_general x2, matrix products, unpack_slots(): jnp.einsum('mr,md->rd', placed, arrived.reshape(-1, width), precision=lax...  2.97 us
  transfers between devices with their start and end apart: 3, of which 2 were waited for; matrix products, arithmetic and copies ran while one was open for 10% of the time, Pallas kernels for 0%

profile of v1, /device:TPU:0, one launch (start us, length us, event | category | flops | bytes accessed | tf_op | source)
XLA Modules:
  0.0 126.1 jit_solution(5945072694557828052)
XLA Ops:
  7.2 0.0 copy-start.8
  7.2 0.0 copy-start.9
  7.2 0.6 copy-done.8
  7.8 0.8 slice_reduce_fusion.1
  8.7 0.1 iota_compare_fusion.2
  8.8 0.6 fusion.6
  9.4 0.6 fusion.10
  10.1 0.6 all_to_all.11
  10.7 6.4 %all-to-all-start = ((f32[8,1,256]{2,1,0:T(1,128)}), f32[8,1,256]{2,1,0:T(1,128)S(1)}, u32[]{:S(2)}, u32[]{:S(2)}) async-start(f32[8,1,256]{2,1,0:T(1,128)} %all_to_all.11), calls=%async_computation | async-start | bytes 16384 | tf_op jit(solution)/shard_map/all_to_all | solution.py:81
  17.0 0.1 broadcast_compare_fusion
  17.1 0.0 copy-done.9
  17.1 1.6 %convolution_multiply_fusion = f32[512,512]{1,0:T(8,128)S(1)} fusion(bf16[1,2,512,512]{3,2,1,0:T(8,128)(2,1)S(1)} %copy-done.9, bf16[1,2,512,512]{3,2,1,0:T(8,128)(2,1)} %param.8), kind=kOutput, calls=%fused_computation | convolution fusion | flops 268697600 | bytes 2097152 | tf_op jit(solution)/shard_map/tr,tc->rc/dot_general | solution.py:65
  18.7 0.0 copy-done.10
  18.7 0.5 convolution_multiply_fusion.1
  19.2 0.0 copy-start.2
  19.2 1.0 copy-done.2
  20.2 0.1 reshape.167
  20.3 0.0 copy-start
  20.3 1.0 reshape.168
  21.3 0.6 copy-done
  21.9 0.9 fusion.4
  22.8 0.3 copy-done.4
  23.1 1.6 %fusion = f32[8,128,128]{2,1,0:T(8,128)S(1)} fusion(f32[8,256,128]{2,1,0:T(8,128)S(1)} %copy-done.4, s32[8,256]{1,0:T(8,128)S(1)} %eq.64, pred[8,256]{1,0:T(8,128)(4,1)S(1)} %broadcast_compare_fusion, pred[8,128]{1,0:T(8,128)(4,1)S(1)} %get-tuple-element.23, f32[8,256,128]{2,1,0:T(8,128)S(1)} %bitcast.56, f32[8,256,128]{2,1,0:T(8,128)S(1)} %reshape.167), kind=kOutput, calls=%fused_computation.7 | convolution fusion | flops 403963904 | bytes 3681280 | tf_op jit(solution)/shard_map/nkr,nrd->nkd/dot_general | solution.py:26
  24.7 1.0 pad_maximum_fusion
  25.8 0.0 all-to-all-done
  25.8 5.2 %all-to-all-start.1 = ((f32[8,256,128]{2,1,0:T(8,128)}), f32[8,256,128]{2,1,0:T(8,128)S(1)}, u32[]{:S(2)}, u32[]{:S(2)}) async-start(f32[8,256,128]{2,1,0:T(8,128)} %pad_maximum_fusion), calls=%async_computation.1 | async-start | bytes 2097152 | tf_op jit(solution)/shard_map/all_to_all | solution.py:78
  31.0 0.0 all-gather.5.cloned.1.call-start
  31.1 0.6 fusion.41
  31.7 0.7 copy-done.6
  32.3 1.3 %compare_reduce_fusion = (pred[256]{0:T(512)(128)(4,1)S(1)}, pred[256]{0:T(512)(128)(4,1)S(1)}) fusion(s32[1,2,256]{2,1,0:T(2,128)S(1)} %copy-done.6, s32[]{:T(128)} %bitcast.18, s32[]{:T(128)} %bitcast), kind=kLoop, calls=%fused_computation.56 | loop fusion | flops 512 | bytes 2568 | tf_op jit(solution)/shard_map/lt | solution.py:41
  33.7 0.0 copy-start.5
  33.7 23.9 %all-to-all-done.1 = f32[8,256,128]{2,1,0:T(8,128)S(1)} async-done(((f32[8,256,128]{2,1,0:T(8,128)}), f32[8,256,128]{2,1,0:T(8,128)S(1)}, u32[]{:S(2)}, u32[]{:S(2)}) %all-to-all-start.1) | async-done | bytes 1048608 | tf_op jit(solution)/shard_map/all_to_all | solution.py:78
  57.6 0.1 fusion.39
  57.7 1.2 convolution_add_fusion.1
  58.8 0.1 select_bitcast_fusion.2
  58.9 1.8 %select_bitcast_fusion = (f32[1,256,128]{2,1,0:T(8,128)}, f32[1,256,128]{2,1,0:T(8,128)S(1)}) fusion(pred[256]{0:T(512)(128)(4,1)S(1)} %get-tuple-element.5, f32[256,128]{1,0:T(8,128)S(1)} %convolution_add_fusion.1, pred[256]{0:T(512)(128)(4,1)S(1)} %get-tuple-element.6, f32[1024,128]{1,0:T(8,128)S(1)} %bitcast.57, f32[256]{0:T(256)S(1)} %iota_convert_fusion, ...), kind=kOutput, calls=%fused_computation.44 | convolution fusion | flops 403046400 | bytes 923136 | tf_op jit(solution)/shard_map/mr,md->rd/dot_general | solution.py:34
  60.8 0.7 pad_maximum_fusion.1
  61.5 0.0 all-gather.5.cloned.1.call-update
  61.5 0.1 reshape.172
  61.6 1.3 %reshape.173 = f32[1,2048,128]{2,1,0:T(8,128)S(1)} reshape(f32[512,512]{1,0:T(8,128)} %copy-done.1) | data formatting | bytes 2097152 | tf_op jit(solution)/shard_map/reshape | solution.py:12
  62.9 0.1 broadcast_bitcast_fusion
  63.0 2.4 %add_select_fusion = f32[1,2048,128]{2,1,0:T(8,128)} fusion(f32[1,2048,128]{2,1,0:T(8,128)S(1)} %reshape.173, f32[1,2048,128]{2,1,0:T(8,128)S(1)} %copy-done, f32[1,2048,128]{2,1,0:T(8,128)S(1)} %reshape.172, pred[2048]{0:T(1024)(128)(4,1)S(1)} %lt.117, pred[2048]{0:T(1024)(128)(4,1)S(1)} %lt.115), kind=kLoop, calls=%fused_computation.6 | loop fusion | flops 1048576 | bytes 4198400 | tf_op jit(solution)/shard_map/jit(_where)/select_n | solution.py:15
  65.4 21.7 %all-gather.5.cloned.1.call-done = f32[8,256,128]{2,1,0:T(8,128)} async-done(((f32[2,256,128]{2,1,0:T(8,128)}), f32[8,256,128]{2,1,0:T(8,128)}) %all-gather.5.cloned.1.call-update) | async-done | bytes 1048592 | tf_op jit(solution)/shard_map/all_gather | solution.py:95
  87.1 1.3 %reduce_sum.9 = bf16[2,256,128]{2,1,0:T(8,128)(2,1)S(1)} reduce(f32[4,2,256,128]{3,2,1,0:T(8,128)} %bitcast.59, f32[]{:T(128)} %constant.1.clone.1), dimensions={0}, to_apply=%region_0.1 | reduce | flops 196608 | bytes 1179652 | tf_op jit(solution)/shard_map/reduce_sum | solution.py:95
  88.4 14.8 %all-gather.1 = bf16[1,2048,128]{2,1,0:T(8,128)(2,1)S(1)} all-gather(bf16[1,256,128]{2,1,0:T(8,128)(2,1)S(1)} %get-tuple-element.11), channel_id=3, replica_groups=mesh['outer'=4,'inner'=8] {'inner'}, dimensions={1}, use_global_device_ids=true | all-gather | bytes 589824 | tf_op jit(solution)/shard_map/all_gather | solution.py:101
  103.2 14.8 %all-gather.2 = bf16[1,2048,128]{2,1,0:T(8,128)(2,1)S(1)} all-gather(bf16[1,256,128]{2,1,0:T(8,128)(2,1)S(1)} %get-tuple-element.12), channel_id=4, replica_groups=mesh['outer'=4,'inner'=8] {'inner'}, dimensions={1}, use_global_device_ids=true | all-gather | bytes 589824 | tf_op jit(solution)/shard_map/all_gather | solution.py:101
  118.0 0.2 multiply_convert_fusion
  118.1 1.1 reshape.171
  (22 shorter events, 0.1 us)
Async XLA Ops:
  7.2 0.7 copy-start.8
  7.2 9.9 %copy-start.9 = (bf16[1,2,512,512]{3,2,1,0:T(8,128)(2,1)S(1)}, bf16[1,2,512,512]{3,2,1,0:T(8,128)(2,1)}, u32[]{:S(2)}) copy-start(bf16[1,2,512,512]{3,2,1,0:T(8,128)(2,1)} %param.9) | copy-start | bytes 3145732
  10.7 15.1 %all-to-all-start = ((f32[8,1,256]{2,1,0:T(1,128)}), f32[8,1,256]{2,1,0:T(1,128)S(1)}, u32[]{:S(2)}, u32[]{:S(2)}) async-start(f32[8,1,256]{2,1,0:T(1,128)} %all_to_all.11), calls=%async_computation | async-start | bytes 16384 | tf_op jit(solution)/shard_map/all_to_all | solution.py:81
  17.1 1.6 %copy-start.10 = (bf16[1,2,512,512]{3,2,1,0:T(8,128)(2,1)S(1)}, bf16[1,2,512,512]{3,2,1,0:T(8,128)(2,1)}, u32[]{:S(2)}) copy-start(bf16[1,2,512,512]{3,2,1,0:T(8,128)(2,1)} %param.8) | copy-start | bytes 3145732
  18.7 1.5 %copy-start.1 = (f32[512,512]{1,0:T(8,128)}, f32[512,512]{1,0:T(8,128)S(1)}, u32[]{:S(2)}) copy-start(f32[512,512]{1,0:T(8,128)S(1)} %convolution_multiply_fusion) | copy-start | bytes 3145732
  19.2 1.0 copy-start.2
  20.3 1.6 %copy-start = (f32[1,2048,128]{2,1,0:T(8,128)S(1)}, f32[1,2048,128]{2,1,0:T(8,128)}, u32[]{:S(2)}) copy-start(f32[1,2048,128]{2,1,0:T(8,128)} %param.10) | copy-start | bytes 3145732
  21.9 1.2 copy-start.4
  25.8 5.3 %copy-start.7 = (s32[1,2]{1,0:T(1,128)S(1)}, s32[1,2]{1,0:T(1,128)}, u32[]{:S(2)}) copy-start(s32[1,2]{1,0:T(1,128)} %param.14) | copy-start | bytes 28
  25.8 31.8 %all-to-all-start.1 = ((f32[8,256,128]{2,1,0:T(8,128)}), f32[8,256,128]{2,1,0:T(8,128)S(1)}, u32[]{:S(2)}, u32[]{:S(2)}) async-start(f32[8,256,128]{2,1,0:T(8,128)} %pad_maximum_fusion), calls=%async_computation.1 | async-start | bytes 2097152 | tf_op jit(solution)/shard_map/all_to_all | solution.py:78
  31.0 56.1 %all-gather.5.cloned.1.call-start = ((), (), s32[]{:S(2)}) async-start(), calls=%async_computation.2 | async-start | bytes 1310720 | tf_op jit(solution)/shard_map/all_gather | solution.py:95
  31.6 0.7 copy-start.6
  33.7 24.0 %copy-start.5 = (f32[1,256,128]{2,1,0:T(8,128)S(1)}, f32[1,256,128]{2,1,0:T(8,128)}, u32[]{:S(2)}) copy-start(f32[1,256,128]{2,1,0:T(8,128)} %param.11) | copy-start | bytes 393220
  58.8 2.7 %copy-start.3 = (f32[512,512]{1,0:T(8,128)S(1)}, f32[512,512]{1,0:T(8,128)}, u32[]{:S(2)}) copy-start(f32[512,512]{1,0:T(8,128)} %copy-done.2) | copy-start | bytes 3145732
Sparse Core Ops, SparseCore 0:
  61.6 25.4 all-gather.4
